TPU v7x, 256 devices: a whole 4x4x8 slice. The times are simulated.
256 devices in a mesh: dp: 32 (over y_hi, z, core), vocab: 8 (over x, y_lo).
Axes of the slice: x: 4, y: 4 (y_hi: 2, y_lo: 2; y = y_hi * 2 + y_lo), z: 8, core: 2. Of those that a mesh axis runs over, the one named last changes fastest.
Arguments:
- hidden: bfloat16 [16384, 3072], P(('dp', 'vocab')), may hold values from -128 to 128
- targets: int32 [16384], P(('dp', 'vocab')), may hold values from 0 to 16383
- lengths: int32 [32], P('dp'), may hold values from 1 to 512
- head: bfloat16 [3072, 16384], P('dp', 'vocab'), may hold values from -1 to 1
Outputs:
- grad_hidden: bfloat16 [16384, 3072], P(('dp', 'vocab'))
- loss: float32 [], replicated
All inputs are finite; a program needn't handle non-finite values.
Results may differ from a plain program's by a relative error of at most 0.0052.
Values may be sent and summed in bfloat16 or wider, within the bound.
A program may use at most 64 MiB of HBM per device.

v0:
```python
import functools

import jax
import jax.numpy as jnp
from jax import lax
from jax.sharding import Mesh
from jax.sharding import PartitionSpec as P

DP = ("dp_0", "dp_1", "dp_2")
VOCAB = ("vocab_0", "vocab_1")
DP_VOCAB = ("dp_0", "dp_1", "dp_2", "vocab_0", "vocab_1")


def whole_of(shard, axes, dim):
    filled = shard
    for number in range(len(axes) - 1, -1, -1):
        filled = lax.all_gather(filled, axes[number], axis=dim, tiled=True)
    return filled


def all_in_one(shard, axis):
    leaves = jax.tree.leaves(shard)
    sequence = sorted(range(len(leaves)), key=lambda k: -leaves[k].size)
    width = (1, *leaves[sequence[0]].shape)[-1]
    lines = [
        jnp.pad(leaves[k].reshape(-1), (0, -leaves[k].size % width)).reshape(-1, width)
        for k in sequence
    ]
    both, at, found = (lax.all_gather(jnp.concatenate(lines), axis), 0, {})
    for k, line in zip(sequence, lines):
        share = both[:, at : at + len(line)].reshape(len(both), -1)
        found[k] = share[:, : leaves[k].size].reshape(-1, *leaves[k].shape)
        at += len(line)
    numbers = iter(range(len(leaves)))
    return jax.tree.map(lambda _: found[next(numbers)], shard)


def combined_all(shard, axis, combine):
    everything = all_in_one(shard, axis)
    first = jax.tree.map(lambda part: part[0], everything)

    def turn(k, so_far):
        return combine(so_far, jax.tree.map(lambda part: part[k], everything))

    return lax.fori_loop(1, lax.axis_size(axis), turn, first)


def one_axis_at_a_time(shard, axes):
    return functools.reduce(lax.psum, axes, shard)


def merge_rows(earlier, later):
    maxima = jnp.maximum(earlier[0], later[0])
    totals = earlier[1] * jnp.exp(earlier[0] - maxima) + later[1] * jnp.exp(later[0] - maxima)
    return (maxima, totals, earlier[2] + later[2])


def local(hidden, targets, lengths, head):
    whole_head, all_lengths = (
        lax.all_gather(head, DP, axis=0, tiled=True),
        lax.all_gather(lengths, DP, axis=0, tiled=True),
    )
    clip_rows, clip_targets = (whole_of(hidden, VOCAB, 0), whole_of(targets, VOCAB, 0))
    level_count = whole_head.shape[1]
    home_rows = hidden.shape[0]
    logits = jnp.dot(clip_rows, whole_head, preferred_element_type=jnp.float32)
    local_levels = clip_targets - lax.axis_index(VOCAB) * level_count
    level_grid = jnp.arange(level_count, dtype=jnp.int32)
    is_target = local_levels[:, None] == level_grid[None, :]
    target_logit = jnp.sum(jnp.where(is_target, logits, 0.0), axis=1)
    maxima = jnp.max(logits, axis=1)
    totals = jnp.sum(jnp.exp(logits - maxima[:, None]), axis=1)
    maxima, totals, target_logit = combined_all((maxima, totals, target_logit), VOCAB, merge_rows)
    log_total = maxima + jnp.log(totals)
    total_count = jnp.sum(all_lengths).astype(jnp.float32)
    clip_index = jnp.arange(all_lengths.shape[0], dtype=jnp.int32)
    clip_length = jnp.sum(jnp.where(clip_index == lax.axis_index(DP), all_lengths, 0))
    positions = jnp.arange(clip_rows.shape[0], dtype=jnp.int32)
    valid_rows = (positions < clip_length).astype(jnp.float32)
    row_loss = valid_rows * (log_total - target_logit)
    home_loss = jnp.sum(
        lax.dynamic_slice_in_dim(row_loss, lax.axis_index(VOCAB) * home_rows, home_rows, 0)
    )
    loss = one_axis_at_a_time(home_loss, DP_VOCAB) / total_count
    weights = (valid_rows / total_count)[:, None]
    grad_logits = (
        weights * (jnp.exp(logits - log_total[:, None]) - is_target.astype(jnp.float32))
    ).astype(jnp.bfloat16)
    grad_home = lax.psum_scatter(
        lax.dot_general(
            grad_logits, whole_head, (((1,), (1,)), ((), ())), preferred_element_type=jnp.float32
        ),
        VOCAB,
        scatter_dimension=0,
        tiled=True,
    )
    return (grad_home.astype(jnp.bfloat16), loss)


def solution(mesh):
    torus = Mesh(
        mesh.devices.reshape(2, 8, 2, 4, 2), ("dp_0", "dp_1", "dp_2", "vocab_0", "vocab_1")
    )
    return jax.shard_map(
        local,
        mesh=torus,
        in_specs=(P(DP_VOCAB, None), P(DP_VOCAB), P(DP), P(DP, VOCAB)),
        out_specs=(P(DP_VOCAB, None), P()),
        check_vma=False,
    )
```

profile of v0, /device:TPU:4, one launch (start us, length us, event | category | flops | bytes accessed | tf_op | source)
XLA Modules:
  0.0 380.6 jit_solution(14241844789752872180)
XLA Ops:
  7.2 13.4 %all_gather.25 = bf16[128,3072]{1,0:T(8,128)(2,1)} all-gather(bf16[64,3072]{1,0:T(8,128)(2,1)} %param.6), channel_id=1, replica_groups=mesh['dp_0'=2,'dp_1'=8,'dp_2'=2,'vocab_0'=4,'vocab_1'=2] {'vocab_1'}, dimensions={0}, use_global_device_ids=true | all-gather | bytes 1179648 | tf_op jit(solution)/shard_map/all_gather | solution.py:17
  20.7 0.7 all-gather.8.cloned.1.call-update
  22.1 1.3 dynamic-slice.1
  23.3 1.2 dynamic-slice
  24.6 0.7 dynamic-update-slice
  25.2 20.8 %all-reduce = s32[32]{0:T(128)S(1)} all-reduce(s32[32]{0:T(128)S(1)} %dynamic-update-slice), channel_id=1, replica_groups=mesh['dp_0'=2,'dp_1'=8,'dp_2'=2,'vocab_0'=4,'vocab_1'=2] {'dp_0','dp_1',..., use_global_device_ids=true, to_apply=%add | all-reduce | flops 32 | bytes 256
  48.0 0.9 dynamic-update-slice.1
  48.8 4.3 %all-reduce.1 = s32[128]{0:T(128)S(1)} all-reduce(s32[128]{0:T(128)S(1)} %dynamic-update-slice.1), channel_id=1, replica_groups=mesh['dp_0'=2,'dp_1'=8,'dp_2'=2,'vocab_0'=4,'vocab_1'=2] {'vocab_1'}, use_global_device_ids=true, to_apply=%add.1 | all-reduce | flops 128 | bytes 1024
  53.1 7.8 %all-gather.1 = s32[4,1,128]{2,1,0:T(1,128)S(1)} all-gather(s32[1,1,128]{2,1,0:T(1,128)S(1)} %bitcast.43), channel_id=1, replica_groups=mesh['dp_0'=2,'dp_1'=8,'dp_2'=2,'vocab_0'=4,'vocab_1'=2] {'vocab_0'}, dimensions={0}, use_global_device_ids=true | all-gather | bytes 2560 | tf_op jit(solution)/shard_map/all_gather | solution.py:17
  61.5 2.9 all-gather.6.cloned.1.call-done
  64.3 121.2 %all-gather.8.cloned.1.call-done = bf16[3072,2048]{1,0:T(8,128)(2,1)} async-done(((bf16[96,2048]{1,0:T(8,128)(2,1)}), bf16[3072,2048]{1,0:T(8,128)(2,1)}) %all-gather.8.cloned.1.call-update) | async-done | bytes 12582928 | tf_op jit(solution)/shard_map/all_gather | solution.py:60
  185.5 10.7 %fusion.8 = (f32[512]{0:T(512)S(1)}, f32[512,2048]{1,0:T(8,128)S(1)}) fusion(bf16[512,3072]{1,0:T(8,128)(2,1)} %all-gather.6.cloned.1.call-done, bf16[3072,2048]{1,0:T(8,128)(2,1)} %all-gather.8.cloned.1.call-done), kind=kOutput, calls=%fused_computation.26 | convolution fusion | flops 6443499008 | bytes 19924992 | tf_op jit(solution)/shard_map/dot_general | solution.py:66
  196.3 2.0 copy-done
  198.3 1.1 exponential_reduce_fusion
  199.4 24.6 %all-gather.2 = f32[8,3,512]{2,1,0:T(4,128)S(1)} all-gather(f32[1,3,512]{2,1,0:T(4,128)S(1)} %maximum_bitcast_fusion), channel_id=2, replica_groups=mesh['dp_0'=2,'dp_1'=8,'dp_2'=2,'vocab_0'=4,'vocab_1'=2] {'vocab_0','voc..., dimensions={0}, use_global_device_ids=true | all-gather | bytes 55296 | tf_op jit(solution)/shard_map/all_gather | solution.py:29
  225.3 13.1 %fusion = f32[512,3072]{1,0:T(8,128)} fusion(bf16[3072,2048]{1,0:T(8,128)(2,1)} %all-gather.8.cloned.1.call-done, f32[512,2048]{1,0:T(8,128)} %copy-done, f32[512]{0:T(512)S(1)} %get-tuple-element.204, s32[512]{0:T(512)S(1)} %bitcast.42, f32[512]{0:T(512)S(1)} %fusion.4), kind=kOutput, calls=%fused_computation.8 | convolution fusion | flops 6448742400 | bytes 23074816 | tf_op jit(solution)/shard_map/dot_general | solution.py:90
  238.4 0.7 dynamic-slice_reduce_fusion
  239.0 7.0 %psum.35 = f32[]{:T(128)} all-reduce(f32[]{:T(128)} %dynamic-slice_reduce_fusion), channel_id=1, replica_groups=mesh['dp_0'=2,'dp_1'=8,'dp_2'=2,'vocab_0'=4,'vocab_1'=2] {'dp_0'}, use_global_device_ids=true, to_apply=%region_9.10 | all-reduce | flops 1 | bytes 8 | tf_op jit(solution)/shard_map/psum | solution.py:49
  246.1 16.7 %psum.36 = f32[]{:T(128)} all-reduce(f32[]{:T(128)} %psum.35), channel_id=1, replica_groups=mesh['dp_0'=2,'dp_1'=8,'dp_2'=2,'vocab_0'=4,'vocab_1'=2] {'dp_1'}, use_global_device_ids=true, to_apply=%region_10.11 | all-reduce | flops 1 | bytes 8 | tf_op jit(solution)/shard_map/psum | solution.py:49
  262.7 3.1 psum.37
  265.8 10.4 %psum.38 = f32[]{:T(128)} all-reduce(f32[]{:T(128)} %psum.37), channel_id=1, replica_groups=mesh['dp_0'=2,'dp_1'=8,'dp_2'=2,'vocab_0'=4,'vocab_1'=2] {'vocab_0'}, use_global_device_ids=true, to_apply=%region_12.13 | all-reduce | flops 1 | bytes 8 | tf_op jit(solution)/shard_map/psum | solution.py:49
  276.2 6.4 %psum.39 = f32[]{:T(128)} all-reduce(f32[]{:T(128)} %psum.38), channel_id=1, replica_groups=mesh['dp_0'=2,'dp_1'=8,'dp_2'=2,'vocab_0'=4,'vocab_1'=2] {'vocab_1'}, use_global_device_ids=true, to_apply=%region_13.14 | all-reduce | flops 1 | bytes 8 | tf_op jit(solution)/shard_map/psum | solution.py:49
  283.3 87.7 %reduce-scatter.2.cloned.1.call-done = f32[64,3072]{1,0:T(8,128)} async-done(((f32[512,3072]{1,0:T(8,128)}), f32[64,3072]{1,0:T(8,128)}) %reduce-scatter.2.cloned.1.call-update) | async-done | bytes 786448 | tf_op jit(solution)/shard_map/reduce_scatter | solution.py:89
  371.0 1.9 convert_element_type.17
  (46 shorter events, 3.0 us)
Async XLA Ops:
  7.2 57.2 %all-gather.6.cloned.1.call-start = ((), (), s32[]{:S(2)}) async-start(), calls=%async_computation.1 | async-start | bytes 3932160 | tf_op jit(solution)/shard_map/all_gather | solution.py:17
  20.6 164.9 %all-gather.8.cloned.1.call-start = ((), (), s32[]{:S(2)}) async-start(), calls=%async_computation.2 | async-start | bytes 12976128 | tf_op jit(solution)/shard_map/all_gather | solution.py:60
  21.4 349.7 %reduce-scatter.2.cloned.1.call-start = ((), (), s32[]{:S(2)}) async-start(), calls=%async_computation.3 | async-start | bytes 7077888 | tf_op jit(solution)/shard_map/reduce_scatter | solution.py:89
  196.2 2.0 copy-start
Sparse Core Ops, SparseCore 0:
  20.7 43.5 all-gather.5
  67.1 118.3 all-gather.7
  238.5 132.4 reduce-scatter.1
where the time goes:
time: 382 us; the launch traced here: 381 us
  waiting for transfers between devices  212 us (55%)
  blocking collectives  114 us (30%)
  matrix products  23.8 us (6%)
  between operations  17.6 us (5%)
  local copies, waits for them, and re-layouts  6.23 us (2%)
  other arithmetic  5.71 us (1%)
    all_gather x1, waiting for transfers between devices, local(): lax.all_gather(head, DP, axis=0, tiled=True)  121 us
    reduce_scatter x1, waiting for transfers between devices, local(): lax.psum_scatter(lax.dot_general(grad_logits, whole_head, (((1,), (1,)),...  87.7 us
    psum x5, blocking collectives, one_axis_at_a_time(): return functools.reduce(lax.psum, axes, shard)  43.6 us
    unnamed x2, blocking collectives  25 us
    all_gather x1, blocking collectives, all_in_one(): both, at, found = (lax.all_gather(jnp.concatenate(lines), axis), 0, {})  24.6 us
    all_gather x2, blocking collectives, whole_of(): filled = lax.all_gather(filled, axes[number], axis=dim, tiled=True)  21.2 us
    dot_general x1, matrix products, local(): lax.dot_general(grad_logits, whole_head, (((1,), (1,)), ((), ())), prefer...  13.1 us
    dot_general x1, matrix products, local(): logits = jnp.dot(clip_rows, whole_head, preferred_element_type=jnp.float32)  10.7 us
  transfers between devices with their start and end apart: 3, of which 3 were waited for; matrix products, arithmetic and copies ran while one was open for 2% of the time, Pallas kernels for 0%

commit v1 on v0

v1 whole, which is shorter than its diff:
```python
import jax
import jax.numpy as jnp
from jax import lax
from jax.experimental import pallas as pl
from jax.experimental.pallas import tpu as pltpu
from jax.sharding import Mesh
from jax.sharding import PartitionSpec as P

AXES = ("yh", "z", "c", "x", "yl")
SIZES = (2, 8, 2, 4, 2)
DP = ("yh", "z", "c")
VOCAB = ("x", "yl")
MESH = pl.DeviceIdType.MESH

WIDTH = 3072
LEVELS = 2048
HOME = 64
ROWS = 512
HEAD_ROWS = 96
PART = 48
HALF = LEVELS // 2
CHUNKS = 6
CHUNK = WIDTH // CHUNKS
PAIR = 384


def kernel(
    hid_ref, aux_ref, head_ref, grad_ref, loss_ref,
    H, X, A, L, G, PT, R1, R2, R3, S2, SY, YR, KEEP, ST, LS, SB,
    zs, zr, ys, yr, cs, cr, hs, hr, as_, ar, ts, tr, ss, sr, rs, rr, ls,
):
    yh, z, c, x, yl = (lax.axis_index(name) for name in AXES)
    oyh, oc, oyl = 1 - yh, 1 - c, 1 - yl
    me = x * 2 + yl

    def remote(src, dst, send, recv, **device):
        return pltpu.make_async_remote_copy(
            src_ref=src, dst_ref=dst, send_sem=send, recv_sem=recv,
            device_id=device, device_id_type=MESH,
        )

    def zdev(d):
        return lax.rem(z + d + 8, 8)

    def xdev(d):
        return lax.rem(x + d + 4, 4)

    vocab_peers = [(dx, dy) for dx in range(4) for dy in range(2) if dx or dy]

    def vpeer(dx, dy):
        return dict(x=xdev(dx), yl=lax.rem(yl + dy, 2))

    def vindex(dx, dy):
        return xdev(-dx) * 2 + lax.rem(yl + dy, 2)

    barrier = pltpu.get_barrier_semaphore()
    peers = [dict(c=oc), dict(yh=oyh)]
    peers += [dict(z=zdev(d)) for d in range(1, 8)]
    peers += [vpeer(dx, dy) for dx, dy in vocab_peers]
    for device in peers:
        pl.semaphore_signal(barrier, 1, device_id=device, device_id_type=MESH)

    def row0(ring, zz, cc):
        return ring * 1536 + zz * 192 + cc * 96

    def head_at(ring, zz, cc, start, size, lanes=None):
        rows = pl.ds(pl.multiple_of(row0(ring, zz, cc) + start, 16), size)
        if lanes is None:
            return H.at[rows, :]
        return H.at[rows, pl.ds(lanes * HALF, HALF)]

    own_copies = [
        pltpu.make_async_copy(head_ref, head_at(yh, z, c, 0, HEAD_ROWS), ls.at[0]),
        pltpu.make_async_copy(hid_ref, X.at[pl.ds(pl.multiple_of(me * HOME, HOME), HOME), :], ls.at[1]),
        pltpu.make_async_copy(aux_ref, A.at[me], ls.at[2]),
    ]
    for copy in own_copies:
        copy.start()
    SB[0, 0] = jnp.broadcast_to(aux_ref[1:2, :].astype(jnp.float32), (8, 128))
    pl.semaphore_wait(barrier, len(peers))

    sent = []

    def send(copy):
        copy.start()
        sent.append(copy)

    def sum_copy(k, stage, d=0):
        if stage == 0:
            return remote(SB.at[k, 0], SB.at[k, 1], ss.at[k, 0], sr.at[k, 0], c=oc)
        if stage == 1:
            return remote(SB.at[k, 2], SB.at[k, 3], ss.at[k, 1], sr.at[k, 1], yh=oyh)
        return remote(
            SB.at[k, 4 + z], SB.at[k, 4 + z], ss.at[k, 1 + d], sr.at[k, 1 + d], z=zdev(d)
        )

    def sum_stage(k, stage):
        if stage == 1:
            sum_copy(k, 0).wait_recv()
            SB[k, 2] = SB[k, 0] + SB[k, 1]
            sum_copy(k, 1).start()
        elif stage == 2:
            sum_copy(k, 1).wait_recv()
            SB[k, 4 + z] = SB[k, 2] + SB[k, 3]
            for d in range(1, 8):
                sum_copy(k, 2, d).start()
        elif stage == 3:
            for d in range(1, 8):
                remote(
                    SB.at[k, 4 + z], SB.at[k, 4 + zdev(-d)], ss.at[k, 1 + d], sr.at[k, 1 + d], z=zdev(d)
                ).wait_recv()
            total = SB[k, 4]
            for n in range(1, 8):
                total = total + SB[k, 4 + n]
            for stage_ in range(2):
                sum_copy(k, stage_).wait_send()
            for d in range(1, 8):
                sum_copy(k, 2, d).wait_send()
            return total

    DIRS = (1, -1)
    B, OWN_A, PEER_A = 0, 1, 2

    def item_at(item, zz, cc, lanes=None):
        if item == B:
            return head_at(yh, zz, cc, PART, PART, lanes)
        return head_at(yh if item == OWN_A else oyh, zz, cc, 0, PART, lanes)

    def lanes_of(step, dr):
        return None if step < 4 else (0 if dr == 0 else 1)

    def z_send(item, step, dr, src=None):
        zz = zdev(-DIRS[dr] * (step - 1))
        there = item_at(item, zz, c, lanes_of(step, dr))
        send(remote(
            there if src is None else src, there,
            zs.at[dr, step - 1, item], zr.at[dr, step - 1, item], z=zdev(DIRS[dr]),
        ))

    def z_wait(item, step, dr):
        here = item_at(item, zdev(-DIRS[dr] * step), c, lanes_of(step, dr))
        remote(
            here, here, zs.at[dr, step - 1, item], zr.at[dr, step - 1, item], z=zdev(DIRS[dr])
        ).wait_recv()
        return here

    def c_send(index, ref, src=None):
        send(remote(ref if src is None else src, ref, cs.at[index], cr.at[index], c=oc))

    def c_wait(index, ref):
        remote(ref, ref, cs.at[index], cr.at[index], c=oc).wait_recv()

    def c_index(item, step, dr):
        return 1 + (dr * 4 + step - 1) * 3 + item

    def y_send(index, ref, src=None):
        send(remote(ref if src is None else src, ref, ys.at[index], yr.at[index], yh=oyh))

    def y_wait(index, ref):
        remote(ref, ref, ys.at[index], yr.at[index], yh=oyh).wait_recv()

    def y_index(step, dr):
        return 2 + dr * 4 + step - 1

    def peer_b(step, dr, cc):
        return head_at(oyh, zdev(-DIRS[dr] * step), cc, PART, PART, lanes_of(step, dr))

    def hid_at(v, half=None):
        if half is None:
            return X.at[pl.ds(pl.multiple_of(v * HOME, HOME), HOME), :]
        return X.at[pl.ds(pl.multiple_of(v * HOME + half * 32, 32), 32), :]

    sum_copy(0, 0).start()
    for n, (dx, dy) in enumerate(vocab_peers):
        send(remote(aux_ref, A.at[me], as_.at[n], ar.at[n], **vpeer(dx, dy)))
    own_a, own_b = head_ref.at[pl.ds(0, PART), :], head_ref.at[pl.ds(PART, PART), :]
    send(remote(hid_ref, hid_at(me), hs.at[0], hr.at[0], yl=oyl))
    y_send(0, head_at(yh, z, c, 0, PART), own_a)
    for dr in range(2):
        z_send(B, 1, dr, own_b)
        send(remote(hid_ref, hid_at(me), hs.at[1 + dr], hr.at[1 + dr], x=xdev(DIRS[dr])))
    y_send(1, head_at(yh, z, c, PART, PART), own_b)
    for dr in range(2):
        z_send(OWN_A, 1, dr, own_a)
    c_send(0, head_at(yh, z, c, 0, HEAD_ROWS), head_ref)

    ref = head_at(oyh, z, c, 0, PART)
    y_wait(0, ref)
    for dr in range(2):
        z_send(PEER_A, 1, dr)
    c_send(25, ref)
    hid_peer = hid_at(x * 2 + oyl)
    remote(hid_peer, hid_peer, hs.at[0], hr.at[0], yl=oyl).wait_recv()
    for dr in range(2):
        send(remote(hid_peer, hid_peer, hs.at[3 + dr], hr.at[3 + dr], x=xdev(DIRS[dr])))
    ref = head_at(oyh, z, c, PART, PART)
    y_wait(1, ref)
    c_send(26, ref)
    sum_stage(0, 1)

    def pass_on(items, step):
        for item in items:
            for dr in range(2):
                here = z_wait(item, step, dr)
                if step < 4:
                    z_send(item, step + 1, dr)
                if item == B:
                    y_send(y_index(step, dr), here)
                c_send(c_index(item, step, dr), here)

    def take_y(step):
        for dr in range(2):
            ref = peer_b(step, dr, c)
            y_wait(y_index(step, dr), ref)
            c_send(27 + dr * 4 + step - 1, ref)

    def take_c(step):
        for dr in range(2):
            for item in range(3):
                c_wait(
                    c_index(item, step, dr),
                    item_at(item, zdev(-DIRS[dr] * step), oc, lanes_of(step, dr)),
                )
            c_wait(27 + dr * 4 + step - 1, peer_b(step, dr, oc))

    def hid_pass(kind):
        for dr in range(2):
            v = xdev(-DIRS[dr]) * 2 + (yl if kind == 0 else oyl)
            ref = hid_at(v)
            n = 1 + 2 * kind + dr
            remote(ref, ref, hs.at[n], hr.at[n], x=xdev(DIRS[dr])).wait_recv()
            half = hid_at(v, dr)
            n = 5 + 2 * kind + dr
            send(remote(half, half, hs.at[n], hr.at[n], x=xdev(DIRS[dr])))

    def hid_far(kind):
        for dr in range(2):
            half = hid_at(xdev(2) * 2 + (yl if kind == 0 else oyl), dr)
            n = 5 + 2 * kind + dr
            remote(half, half, hs.at[n], hr.at[n], x=xdev(DIRS[dr])).wait_recv()

    def multiply(q, first=False):
        pair = lax.rem(lax.div(z, 2) + q, 4)
        for ring in range(2):
            start = pl.multiple_of(ring * 1536 + pair * PAIR, 128)

            def tile(n, carry, start=start, fresh=first and ring == 0):
                at = pl.ds(pl.multiple_of(n * 256, 256), 256)
                part = jnp.dot(
                    X[:, pl.ds(start, PAIR)], H[pl.ds(start, PAIR), at],
                    preferred_element_type=jnp.float32,
                )
                if fresh:
                    L[:, at] = part
                else:
                    L[:, at] += part
                return carry

            lax.fori_loop(0, LEVELS // 256, tile, 0)

    pass_on((B, OWN_A, PEER_A), 1)
    hid_pass(0)
    pass_on((B, OWN_A, PEER_A), 2)
    take_y(1)
    hid_pass(1)
    sum_stage(0, 2)
    pass_on((B, OWN_A, PEER_A), 3)
    take_y(2)
    for copy in own_copies:
        copy.wait()
    c_wait(0, head_at(yh, z, oc, 0, HEAD_ROWS))
    c_wait(25, head_at(oyh, z, oc, 0, PART))
    c_wait(26, head_at(oyh, z, oc, PART, PART))
    take_c(1)
    hid_far(0)
    hid_far(1)
    for n, (dx, dy) in enumerate(vocab_peers):
        there = A.at[vindex(dx, dy)]
        remote(aux_ref, there, as_.at[n], ar.at[n], **vpeer(dx, dy)).wait_recv()
    multiply(0, first=True)
    take_y(3)
    take_c(2)
    take_c(3)
    multiply(1)
    pass_on((B,), 4)
    multiply(3)
    pass_on((OWN_A, PEER_A), 4)
    take_y(4)
    count_tile = sum_stage(0, 3)
    take_c(4)
    multiply(2)

    base = me * LEVELS
    lane = lax.broadcasted_iota(jnp.int32, (HOME, 128), 1)
    eye = lane == lax.broadcasted_iota(jnp.int32, (HOME, 128), 0)
    level = lax.broadcasted_iota(jnp.int32, (HOME, LEVELS), 1)

    def to_row(column):
        return jnp.sum(jnp.where(eye, column, 0.0), axis=0, keepdims=True)

    def to_column(row):
        return jnp.sum(jnp.where(eye, row, 0.0), axis=1, keepdims=True)

    def target_of(v):
        row = A[v][0:1, :].astype(jnp.float32)
        return to_column(row).astype(jnp.int32) - base

    def rows_of(v):
        return pl.ds(pl.multiple_of(v * HOME, HOME), HOME)

    def statistics(v, carry):
        logits = L[rows_of(v), :]
        top = jnp.max(logits, axis=1, keepdims=True)
        total = jnp.sum(jnp.exp(logits - top), axis=1, keepdims=True)
        hit = jnp.sum(jnp.where(level == target_of(v), logits, 0.0), axis=1, keepdims=True)
        for n, column in enumerate((top, total, hit)):
            ST[me, n, pl.ds(v, 1), :] = to_row(column)
        return carry

    lax.fori_loop(0, 8, statistics, 0)
    for n, (dx, dy) in enumerate(vocab_peers):
        send(remote(ST.at[me], ST.at[me], ts.at[n], tr.at[n], **vpeer(dx, dy)))
    for n, (dx, dy) in enumerate(vocab_peers):
        there = ST.at[vindex(dx, dy)]
        remote(ST.at[me], there, ts.at[n], tr.at[n], **vpeer(dx, dy)).wait_recv()

    top = ST[0, 0]
    for v in range(1, 8):
        top = jnp.maximum(top, ST[v, 0])
    total = jnp.zeros((8, 128), jnp.float32)
    hit = jnp.zeros((8, 128), jnp.float32)
    for v in range(8):
        total = total + ST[v, 1] * jnp.exp(ST[v, 0] - top)
        hit = hit + ST[v, 2]
    log_total = top + jnp.log(total)
    LS[...] = log_total

    length = aux_ref[1:2, 0:1]
    lane8 = lax.broadcasted_iota(jnp.int32, (8, 128), 1)
    place = lax.broadcasted_iota(jnp.int32, (8, 128), 0) * HOME + lane8
    counted = (lane8 < HOME) & (place < length)
    row_loss = jnp.where(counted, log_total - hit, 0.0)
    clip_loss = jnp.sum(jnp.sum(row_loss, axis=1, keepdims=True), axis=0, keepdims=True)
    SB[1, 0] = jnp.broadcast_to(clip_loss, (8, 128))
    count = count_tile[0:1, 0:1]

    def gradient(v, carry):
        place = v * HOME + lax.broadcasted_iota(jnp.int32, (HOME, 1), 0)
        weight = jnp.where(place < length, 1.0, 0.0) / count
        share = jnp.exp(L[rows_of(v), :] - to_column(LS[pl.ds(v, 1), :]))
        share = share - jnp.where(level == target_of(v), 1.0, 0.0)
        G[rows_of(v), :] = (weight * share).astype(jnp.bfloat16)
        return carry

    lax.fori_loop(0, 8, gradient, 0)
    sum_copy(1, 0).start()

    def block(j, xx):
        return PT.at[j, pl.ds(pl.multiple_of(xx * 128, 128), 128), :]

    def scatter(j, kind):
        d = 1 - 2 * lax.rem(j, 2)
        if kind == 0:
            return remote(block(j, xdev(2)), R1.at[j], rs.at[0, j], rr.at[0, j], x=xdev(d))
        if kind == 1:
            return remote(block(j, xdev(-d)), R2.at[j], rs.at[1, j], rr.at[1, j], x=xdev(-d))
        if kind == 2:
            return remote(S2.at[j], R3.at[j], rs.at[2, j], rr.at[2, j], x=xdev(d))
        return remote(SY.at[j], YR.at[j], rs.at[3, j], rr.at[3, j], yl=oyl)

    def f32(value):
        return value.astype(jnp.float32)

    def scatter_step(j, carry):
        @pl.when(j < CHUNKS)
        def _():
            for n in range(2):
                rows = pl.ds(pl.multiple_of(j * CHUNK + n * 256, 256), 256)
                PT[j, :, n * 256 : (n + 1) * 256] = lax.dot_general(
                    G[...], H[rows, :], (((1,), (1,)), ((), ())),
                    preferred_element_type=jnp.float32,
                ).astype(jnp.bfloat16)
            scatter(j, 0).start()
            scatter(j, 1).start()

        @pl.when((j >= 1) & (j < CHUNKS + 1))
        def _():
            k = j - 1
            d = 1 - 2 * lax.rem(k, 2)
            scatter(k, 0).wait_recv()
            mine = PT[k, pl.ds(pl.multiple_of(xdev(d) * 128, 128), 128), :]
            S2[k] = (f32(R1[k]) + f32(mine)).astype(jnp.bfloat16)
            scatter(k, 2).start()

        @pl.when((j >= 2) & (j < CHUNKS + 2))
        def _():
            k = j - 2
            scatter(k, 1).wait_recv()
            scatter(k, 2).wait_recv()

            def total_of(which):
                mine = PT[k, pl.ds(pl.multiple_of(x * 128 + which * HOME, HOME), HOME), :]
                half = pl.ds(pl.multiple_of(which * HOME, HOME), HOME)
                return f32(mine) + f32(R2[k, half, :]) + f32(R3[k, half, :])

            SY[k] = total_of(oyl).astype(jnp.bfloat16)
            scatter(k, 3).start()
            KEEP[k] = total_of(yl)

        @pl.when(j >= 3)
        def _():
            k = j - 3
            scatter(k, 3).wait_recv()
            at = pl.ds(pl.multiple_of(k * CHUNK, CHUNK), CHUNK)
            grad_ref[:, at] = (KEEP[k] + f32(YR[k])).astype(jnp.bfloat16)

        @pl.when(j == 2)
        def _():
            sum_stage(1, 1)

        @pl.when(j == 4)
        def _():
            sum_stage(1, 2)

        return carry

    lax.fori_loop(0, CHUNKS + 3, scatter_step, 0)

    loss_ref[...] = sum_stage(1, 3) / count_tile
    for copy in sent:
        copy.wait_send()

    def drain(j, carry):
        for kind in range(4):
            scatter(j, kind).wait_send()
        return carry

    lax.fori_loop(0, CHUNKS, drain, 0)


def local(hidden, targets, lengths, head):
    aux = jnp.concatenate(
        [
            jnp.pad(targets, (0, 128 - HOME)).reshape(1, 128),
            jnp.broadcast_to(lengths.reshape(1, 1), (7, 128)),
        ]
    )
    bf16, f32, i32 = jnp.bfloat16, jnp.float32, jnp.int32
    vmem = pl.BlockSpec(memory_space=pltpu.VMEM)
    dma = pltpu.SemaphoreType.DMA
    grad, loss = pl.pallas_call(
        kernel,
        out_shape=(
            jax.ShapeDtypeStruct((HOME, WIDTH), bf16),
            jax.ShapeDtypeStruct((8, 128), f32),
        ),
        in_specs=[vmem] * 3,
        out_specs=(vmem, vmem),
        scratch_shapes=[
            pltpu.VMEM((WIDTH, LEVELS), bf16),
            pltpu.VMEM((ROWS, WIDTH), bf16),
            pltpu.VMEM((8, 8, 128), i32),
            pltpu.VMEM((ROWS, LEVELS), f32),
            pltpu.VMEM((ROWS, LEVELS), bf16),
            pltpu.VMEM((CHUNKS, ROWS, CHUNK), bf16),
            pltpu.VMEM((CHUNKS, 128, CHUNK), bf16),
            pltpu.VMEM((CHUNKS, 128, CHUNK), bf16),
            pltpu.VMEM((CHUNKS, 128, CHUNK), bf16),
            pltpu.VMEM((CHUNKS, 128, CHUNK), bf16),
            pltpu.VMEM((CHUNKS, HOME, CHUNK), bf16),
            pltpu.VMEM((CHUNKS, HOME, CHUNK), bf16),
            pltpu.VMEM((CHUNKS, HOME, CHUNK), f32),
            pltpu.VMEM((8, 3, 8, 128), f32),
            pltpu.VMEM((8, 128), f32),
            pltpu.VMEM((2, 12, 8, 128), f32),
            dma((2, 4, 3)), dma((2, 4, 3)),
            dma((10,)), dma((10,)),
            dma((35,)), dma((35,)),
            dma((9,)), dma((9,)),
            dma((7,)), dma((7,)),
            dma((7,)), dma((7,)),
            dma((2, 9)), dma((2, 9)),
            dma((4, CHUNKS)), dma((4, CHUNKS)),
            dma((3,)),
        ],
        compiler_params=pltpu.CompilerParams(
            collective_id=0, has_side_effects=True, vmem_limit_bytes=58 * 2**20
        ),
    )(hidden, aux, head)
    return grad, loss[0, 0]


def solution(mesh):
    torus = Mesh(mesh.devices.reshape(SIZES), AXES)
    return jax.shard_map(
        local,
        mesh=torus,
        in_specs=(P(DP + VOCAB, None), P(DP + VOCAB), P(DP), P(DP, VOCAB)),
        out_specs=(P(DP + VOCAB, None), P()),
        check_vma=False,
    )
```

time: 382 us -> 132 us (0.35)
  waiting for transfers between devices: 212 us -> 0 us
  Pallas kernels: 0 us -> 127 us
  blocking collectives: 114 us -> 0 us
  matrix products: 23.8 us -> 0 us
  between operations: 17.6 us -> 1.29 us
  other arithmetic: 5.71 us -> 0 us
    pallas_call x0 -> x1, Pallas kernels: none -> 127 us  [local(): pl.pallas_call(kernel, out_shape=(jax.ShapeDtypeStruct((HOME, WIDTH), bf1...]
    all_gather x2 -> x0, waiting for transfers between devices: 124 us -> none  [the longest x1 121 us: local(): lax.all_gather(head, DP, axis=0, tiled=True)]
    reduce_scatter x1 -> x0, waiting for transfers between devices: 87.7 us -> none  [local(): lax.psum_scatter(lax.dot_general(grad_logits, whole_head, (((1,), (1,)),...]
    all_gather x3 -> x0, blocking collectives: 45.8 us -> none  [the longest x1 24.6 us: all_in_one(): both, at, found = (lax.all_gather(jnp.concatenate(lines), axis), 0, {})]
    psum x5 -> x0, blocking collectives: 43.6 us -> none  [one_axis_at_a_time(): return functools.reduce(lax.psum, axes, shard)]
    unnamed x2 -> x0, blocking collectives: 25 us -> none
    dot_general x2 -> x0, matrix products: 23.8 us -> none  [the longest x1 13.1 us: local(): lax.dot_general(grad_logits, whole_head, (((1,), (1,)), ((), ())), prefer...]
  transfers between devices with their start and end apart: 3 -> 0, of which waited for: 3 -> 0; matrix products, arithmetic and copies ran while one was open for 2% -> 0% of each run, Pallas kernels for 0% -> 0%
where the time goes in v1:
time: 132 us
  Pallas kernels  127 us (96%)
  local copies, waits for them, and re-layouts  4.21 us (3%)
    pallas_call x1, Pallas kernels, local(): pl.pallas_call(kernel, out_shape=(jax.ShapeDtypeStruct((HOME, WIDTH), bf1...  127 us

profile of v1, /device:TPU:4, one launch (start us, length us, event | category | flops | bytes accessed | tf_op | source)
XLA Modules:
  0.0 132.2 jit_solution(14954476786242638598)
XLA Ops:
  1.3 0.0 copy-start
  1.3 0.6 copy-done
  1.9 0.6 concatenate.3.aux_ref
  2.5 126.7 %shard_map.59 = (bf16[64,3072]{1,0:T(8,128)(2,1)}, f32[8,128]{1,0:T(8,128)}) custom-call(bf16[64,3072]{1,0:T(8,128)(2,1)} %hid_ref.1, s32[8,128]{1,0:T(8,128)} %concatenate.3.aux_ref, bf16[96,2048]{1,0:T(8,128)(2,1)} %head_ref.1), custom_call_target="tpu_custom_call" | custom-call | tf_op jit(solution)/shard_map/pallas_call | solution.py:451
  129.2 1.2 slice.3
  130.4 1.8 %copy.8 = bf16[64,3072]{1,0:T(8,128)(2,1)} copy(bf16[64,3072]{1,0:T(8,128)(2,1)} %get-tuple-element.8) | data formatting | bytes 786432
  (1 shorter events, 0.0 us)
Async XLA Ops:
  1.3 0.7 copy-start

commit v2 on v1

--- a/solution.py
+++ b/solution.py
@@ -21,13 +21,14 @@
 HALF = LEVELS // 2
 CHUNKS = 6
 CHUNK = WIDTH // CHUNKS
-PAIR = 384
+QUAD = 768
+XC, YC = 4, 2
 
 
 def kernel(
-    hid_ref, aux_ref, head_ref, grad_ref, loss_ref,
-    H, X, A, L, G, PT, R1, R2, R3, S2, SY, YR, KEEP, ST, LS, SB,
-    zs, zr, ys, yr, cs, cr, hs, hr, as_, ar, ts, tr, ss, sr, rs, rr, ls,
+    hid_ref, tgt_ref, len_ref, head_ref, grad_ref, loss_ref,
+    H, X, A, L, G, PT, XR1, XR2, XR3, XS2, SY, YR, YF, SA, YR1, YR2, YR3, YS2, ST, LS, SB,
+    zs, zr, ys, yr, cs, cr, hs, hr, as_, ar, ts, tr, ss, sr, xs, xr, ws, wr, ls,
 ):
     yh, z, c, x, yl = (lax.axis_index(name) for name in AXES)
     oyh, oc, oyl = 1 - yh, 1 - c, 1 - yl
@@ -72,11 +73,11 @@
     own_copies = [
         pltpu.make_async_copy(head_ref, head_at(yh, z, c, 0, HEAD_ROWS), ls.at[0]),
         pltpu.make_async_copy(hid_ref, X.at[pl.ds(pl.multiple_of(me * HOME, HOME), HOME), :], ls.at[1]),
-        pltpu.make_async_copy(aux_ref, A.at[me], ls.at[2]),
+        pltpu.make_async_copy(tgt_ref, A.at[me], ls.at[2]),
     ]
     for copy in own_copies:
         copy.start()
-    SB[0, 0] = jnp.broadcast_to(aux_ref[1:2, :].astype(jnp.float32), (8, 128))
+    SB[0, 0] = jnp.full((8, 128), len_ref[0], jnp.int32).astype(jnp.float32)
     pl.semaphore_wait(barrier, len(peers))
 
     sent = []
@@ -172,31 +173,17 @@
 
     sum_copy(0, 0).start()
     for n, (dx, dy) in enumerate(vocab_peers):
-        send(remote(aux_ref, A.at[me], as_.at[n], ar.at[n], **vpeer(dx, dy)))
+        send(remote(tgt_ref, A.at[me], as_.at[n], ar.at[n], **vpeer(dx, dy)))
     own_a, own_b = head_ref.at[pl.ds(0, PART), :], head_ref.at[pl.ds(PART, PART), :]
-    send(remote(hid_ref, hid_at(me), hs.at[0], hr.at[0], yl=oyl))
     y_send(0, head_at(yh, z, c, 0, PART), own_a)
+    for item, own in ((B, own_b), (OWN_A, own_a)):
+        for dr in range(2):
+            z_send(item, 1, dr, own)
     for dr in range(2):
-        z_send(B, 1, dr, own_b)
         send(remote(hid_ref, hid_at(me), hs.at[1 + dr], hr.at[1 + dr], x=xdev(DIRS[dr])))
     y_send(1, head_at(yh, z, c, PART, PART), own_b)
-    for dr in range(2):
-        z_send(OWN_A, 1, dr, own_a)
+    send(remote(hid_ref, hid_at(me), hs.at[0], hr.at[0], yl=oyl))
     c_send(0, head_at(yh, z, c, 0, HEAD_ROWS), head_ref)
-
-    ref = head_at(oyh, z, c, 0, PART)
-    y_wait(0, ref)
-    for dr in range(2):
-        z_send(PEER_A, 1, dr)
-    c_send(25, ref)
-    hid_peer = hid_at(x * 2 + oyl)
-    remote(hid_peer, hid_peer, hs.at[0], hr.at[0], yl=oyl).wait_recv()
-    for dr in range(2):
-        send(remote(hid_peer, hid_peer, hs.at[3 + dr], hr.at[3 + dr], x=xdev(DIRS[dr])))
-    ref = head_at(oyh, z, c, PART, PART)
-    y_wait(1, ref)
-    c_send(26, ref)
-    sum_stage(0, 1)
 
     def pass_on(items, step):
         for item in items:
@@ -214,14 +201,15 @@
             y_wait(y_index(step, dr), ref)
             c_send(27 + dr * 4 + step - 1, ref)
 
-    def take_c(step):
+    def take_c(step, own):
         for dr in range(2):
-            for item in range(3):
+            for item in (B, OWN_A) if own else (PEER_A,):
                 c_wait(
                     c_index(item, step, dr),
                     item_at(item, zdev(-DIRS[dr] * step), oc, lanes_of(step, dr)),
                 )
-            c_wait(27 + dr * 4 + step - 1, peer_b(step, dr, oc))
+            if not own:
+                c_wait(27 + dr * 4 + step - 1, peer_b(step, dr, oc))
 
     def hid_pass(kind):
         for dr in range(2):
@@ -239,56 +227,79 @@
             n = 5 + 2 * kind + dr
             remote(half, half, hs.at[n], hr.at[n], x=xdev(DIRS[dr])).wait_recv()
 
-    def multiply(q, first=False):
-        pair = lax.rem(lax.div(z, 2) + q, 4)
-        for ring in range(2):
-            start = pl.multiple_of(ring * 1536 + pair * PAIR, 128)
-
-            def tile(n, carry, start=start, fresh=first and ring == 0):
-                at = pl.ds(pl.multiple_of(n * 256, 256), 256)
-                part = jnp.dot(
-                    X[:, pl.ds(start, PAIR)], H[pl.ds(start, PAIR), at],
-                    preferred_element_type=jnp.float32,
-                )
-                if fresh:
-                    L[:, at] = part
-                else:
-                    L[:, at] += part
-                return carry
-
-            lax.fori_loop(0, LEVELS // 256, tile, 0)
-
-    pass_on((B, OWN_A, PEER_A), 1)
+    def multiply(quad, ring, fresh=False):
+        start = pl.multiple_of(ring * 1536 + quad * QUAD, 256)
+
+        def tile(n, carry):
+            at = pl.ds(pl.multiple_of(n * 512, 512), 512)
+            part = jnp.dot(
+                X[:, pl.ds(start, QUAD)], H[pl.ds(start, QUAD), at],
+                preferred_element_type=jnp.float32,
+            )
+            if fresh:
+                L[:, at] = part
+            else:
+                L[:, at] += part
+            return carry
+
+        lax.fori_loop(0, LEVELS // 512, tile, 0)
+
+    near = lax.div(z, 4)
+    far = 1 - near
+
+    pass_on((B,), 1)
+    ref = head_at(oyh, z, c, 0, PART)
+    y_wait(0, ref)
+    for dr in range(2):
+        z_send(PEER_A, 1, dr)
+    c_send(25, ref)
+    pass_on((OWN_A,), 1)
+    sum_stage(0, 1)
     hid_pass(0)
-    pass_on((B, OWN_A, PEER_A), 2)
+    ref = head_at(oyh, z, c, PART, PART)
+    y_wait(1, ref)
+    c_send(26, ref)
+    pass_on((B,), 2)
+    hid_peer = hid_at(x * 2 + oyl)
+    remote(hid_peer, hid_peer, hs.at[0], hr.at[0], yl=oyl).wait_recv()
+    for dr in range(2):
+        send(remote(hid_peer, hid_peer, hs.at[3 + dr], hr.at[3 + dr], x=xdev(DIRS[dr])))
+    pass_on((PEER_A,), 1)
+    pass_on((OWN_A,), 2)
     take_y(1)
+    sum_stage(0, 2)
+    pass_on((B,), 3)
     hid_pass(1)
-    sum_stage(0, 2)
-    pass_on((B, OWN_A, PEER_A), 3)
+    pass_on((PEER_A,), 2)
+    pass_on((OWN_A,), 3)
     take_y(2)
+    pass_on((B,), 4)
     for copy in own_copies:
         copy.wait()
+    for n, (dx, dy) in enumerate(vocab_peers):
+        there = A.at[vindex(dx, dy)]
+        remote(tgt_ref, there, as_.at[n], ar.at[n], **vpeer(dx, dy)).wait_recv()
     c_wait(0, head_at(yh, z, oc, 0, HEAD_ROWS))
+    hid_far(0)
+    hid_far(1)
+    for step in (1, 2, 3):
+        take_c(step, True)
+    multiply(near, yh, True)
+    pass_on((PEER_A,), 3)
+    pass_on((OWN_A,), 4)
+    take_y(3)
+    take_c(4, True)
+    multiply(far, yh)
+    pass_on((PEER_A,), 4)
     c_wait(25, head_at(oyh, z, oc, 0, PART))
     c_wait(26, head_at(oyh, z, oc, PART, PART))
-    take_c(1)
-    hid_far(0)
-    hid_far(1)
-    for n, (dx, dy) in enumerate(vocab_peers):
-        there = A.at[vindex(dx, dy)]
-        remote(aux_ref, there, as_.at[n], ar.at[n], **vpeer(dx, dy)).wait_recv()
-    multiply(0, first=True)
-    take_y(3)
-    take_c(2)
-    take_c(3)
-    multiply(1)
-    pass_on((B,), 4)
-    multiply(3)
-    pass_on((OWN_A, PEER_A), 4)
+    for step in (1, 2, 3):
+        take_c(step, False)
+    multiply(near, oyh)
     take_y(4)
     count_tile = sum_stage(0, 3)
-    take_c(4)
-    multiply(2)
+    take_c(4, False)
+    multiply(far, oyh)
 
     base = me * LEVELS
     lane = lax.broadcasted_iota(jnp.int32, (HOME, 128), 1)
@@ -302,8 +313,8 @@
         return jnp.sum(jnp.where(eye, row, 0.0), axis=1, keepdims=True)
 
     def target_of(v):
-        row = A[v][0:1, :].astype(jnp.float32)
-        return to_column(row).astype(jnp.int32) - base
+        row = A[v].astype(jnp.float32)
+        return jnp.sum(jnp.where(eye[:, :HOME], row, 0.0), axis=1, keepdims=True).astype(jnp.int32) - base
 
     def rows_of(v):
         return pl.ds(pl.multiple_of(v * HOME, HOME), HOME)
@@ -335,7 +346,7 @@
     log_total = top + jnp.log(total)
     LS[...] = log_total
 
-    length = aux_ref[1:2, 0:1]
+    length = len_ref[0]
     lane8 = lax.broadcasted_iota(jnp.int32, (8, 128), 1)
     place = lax.broadcasted_iota(jnp.int32, (8, 128), 0) * HOME + lane8
     counted = (lane8 < HOME) & (place < length)
@@ -355,121 +366,163 @@
     lax.fori_loop(0, 8, gradient, 0)
     sum_copy(1, 0).start()
 
-    def block(j, xx):
-        return PT.at[j, pl.ds(pl.multiple_of(xx * 128, 128), 128), :]
-
-    def scatter(j, kind):
-        d = 1 - 2 * lax.rem(j, 2)
-        if kind == 0:
-            return remote(block(j, xdev(2)), R1.at[j], rs.at[0, j], rr.at[0, j], x=xdev(d))
-        if kind == 1:
-            return remote(block(j, xdev(-d)), R2.at[j], rs.at[1, j], rr.at[1, j], x=xdev(-d))
-        if kind == 2:
-            return remote(S2.at[j], R3.at[j], rs.at[2, j], rr.at[2, j], x=xdev(d))
-        return remote(SY.at[j], YR.at[j], rs.at[3, j], rr.at[3, j], yl=oyl)
-
     def f32(value):
         return value.astype(jnp.float32)
 
-    def scatter_step(j, carry):
-        @pl.when(j < CHUNKS)
-        def _():
-            for n in range(2):
-                rows = pl.ds(pl.multiple_of(j * CHUNK + n * 256, 256), 256)
-                PT[j, :, n * 256 : (n + 1) * 256] = lax.dot_general(
-                    G[...], H[rows, :], (((1,), (1,)), ((), ())),
-                    preferred_element_type=jnp.float32,
-                ).astype(jnp.bfloat16)
-            scatter(j, 0).start()
-            scatter(j, 1).start()
-
-        @pl.when((j >= 1) & (j < CHUNKS + 1))
-        def _():
-            k = j - 1
-            d = 1 - 2 * lax.rem(k, 2)
-            scatter(k, 0).wait_recv()
-            mine = PT[k, pl.ds(pl.multiple_of(xdev(d) * 128, 128), 128), :]
-            S2[k] = (f32(R1[k]) + f32(mine)).astype(jnp.bfloat16)
-            scatter(k, 2).start()
-
-        @pl.when((j >= 2) & (j < CHUNKS + 2))
-        def _():
-            k = j - 2
-            scatter(k, 1).wait_recv()
-            scatter(k, 2).wait_recv()
-
-            def total_of(which):
-                mine = PT[k, pl.ds(pl.multiple_of(x * 128 + which * HOME, HOME), HOME), :]
-                half = pl.ds(pl.multiple_of(which * HOME, HOME), HOME)
-                return f32(mine) + f32(R2[k, half, :]) + f32(R3[k, half, :])
-
-            SY[k] = total_of(oyl).astype(jnp.bfloat16)
-            scatter(k, 3).start()
-            KEEP[k] = total_of(yl)
-
-        @pl.when(j >= 3)
-        def _():
-            k = j - 3
-            scatter(k, 3).wait_recv()
-            at = pl.ds(pl.multiple_of(k * CHUNK, CHUNK), CHUNK)
-            grad_ref[:, at] = (KEEP[k] + f32(YR[k])).astype(jnp.bfloat16)
-
-        @pl.when(j == 2)
-        def _():
-            sum_stage(1, 1)
-
-        @pl.when(j == 4)
-        def _():
-            sum_stage(1, 2)
-
-        return carry
-
-    lax.fori_loop(0, CHUNKS + 3, scatter_step, 0)
-
-    loss_ref[...] = sum_stage(1, 3) / count_tile
+    def turn(j):
+        return 1 if j % 2 else -1
+
+    def compute(j):
+        rows = pl.ds(j * CHUNK, CHUNK)
+        product = lax.dot_general(
+            G[...], H[rows, :], (((1,), (1,)), ((), ())), preferred_element_type=jnp.float32
+        )
+        PT[j] = product.astype(jnp.bfloat16).reshape(4, 2, HOME, CHUNK)
+
+    def write(j, value):
+        grad_ref[:, j * CHUNK : (j + 1) * CHUNK] = value.astype(jnp.bfloat16)
+
+    def y_copy(j, kind):
+        d = turn(j)
+        if kind == 0:
+            return remote(PT.at[j, :, oyl], YF.at[j], ws.at[0, j], wr.at[0, j], yl=oyl)
+        if kind == 1:
+            return remote(SA.at[j, 0], YR1.at[j], ws.at[1, j], wr.at[1, j], x=xdev(d))
+        if kind == 2:
+            return remote(SA.at[j, 1], YR2.at[j], ws.at[2, j], wr.at[2, j], x=xdev(-d))
+        return remote(YS2.at[j], YR3.at[j], ws.at[3, j], wr.at[3, j], x=xdev(d))
+
+    def y_sum(j, xx):
+        return f32(PT[j, xx, yl]) + f32(YF[j, xx])
+
+    def y_first(j):
+        y_copy(j, 0).wait_recv()
+        SA[j, 0] = y_sum(j, xdev(2)).astype(jnp.bfloat16)
+        SA[j, 1] = y_sum(j, xdev(-turn(j))).astype(jnp.bfloat16)
+        y_copy(j, 1).start()
+        y_copy(j, 2).start()
+
+    def y_second(j):
+        y_copy(j, 1).wait_recv()
+        YS2[j] = (y_sum(j, xdev(turn(j))) + f32(YR1[j])).astype(jnp.bfloat16)
+        y_copy(j, 3).start()
+
+    def y_last(j):
+        y_copy(j, 2).wait_recv()
+        y_copy(j, 3).wait_recv()
+        write(j, y_sum(j, x) + f32(YR2[j]) + f32(YR3[j]))
+
+    def x_copy(j, kind):
+        d, k = turn(j), j - YC
+        if kind == 0:
+            return remote(PT.at[j, xdev(2)], XR1.at[k], xs.at[0, k], xr.at[0, k], x=xdev(d))
+        if kind == 1:
+            return remote(PT.at[j, xdev(-d)], XR2.at[k], xs.at[1, k], xr.at[1, k], x=xdev(-d))
+        if kind == 2:
+            return remote(XS2.at[k], XR3.at[k], xs.at[2, k], xr.at[2, k], x=xdev(d))
+        return remote(SY.at[k], YR.at[k], xs.at[3, k], xr.at[3, k], yl=oyl)
+
+    def x_first(j):
+        x_copy(j, 0).start()
+        x_copy(j, 1).start()
+
+    def x_second(j):
+        k = j - YC
+        x_copy(j, 0).wait_recv()
+        XS2[k] = (f32(PT[j, xdev(turn(j))]) + f32(XR1[k])).astype(jnp.bfloat16)
+        x_copy(j, 2).start()
+
+    def x_sum(j, which):
+        k = j - YC
+        return f32(PT[j, x, which]) + f32(XR2[k, which]) + f32(XR3[k, which])
+
+    def x_third(j):
+        k = j - YC
+        x_copy(j, 1).wait_recv()
+        x_copy(j, 2).wait_recv()
+        SY[k] = x_sum(j, oyl).astype(jnp.bfloat16)
+        x_copy(j, 3).start()
+
+    def x_last(j):
+        x_copy(j, 3).wait_recv()
+        write(j, x_sum(j, yl) + f32(YR[j - YC]))
+
+    compute(0)
+    y_copy(0, 0).start()
+    compute(1)
+    y_copy(1, 0).start()
+    compute(2)
+    x_first(2)
+    compute(3)
+    x_first(3)
+    sum_stage(1, 1)
+    compute(4)
+    compute(5)
+    x_second(2)
+    y_first(0)
+    x_first(4)
+    x_second(3)
+    sum_stage(1, 2)
+    y_second(0)
+    x_first(5)
+    y_first(1)
+    x_second(4)
+    x_third(2)
+    x_third(3)
+    y_second(1)
+    x_second(5)
+    y_last(0)
+    x_third(4)
+    x_last(2)
+    x_last(3)
+    x_third(5)
+    y_last(1)
+    x_last(4)
+
+    loss = sum_stage(1, 3) / count_tile
+    loss_ref[0, 0] = loss[0, 0]
+    x_last(5)
     for copy in sent:
         copy.wait_send()
-
-    def drain(j, carry):
-        for kind in range(4):
-            scatter(j, kind).wait_send()
-        return carry
-
-    lax.fori_loop(0, CHUNKS, drain, 0)
+    for kind in range(4):
+        for j in range(YC):
+            y_copy(j, kind).wait_send()
+        for j in range(YC, CHUNKS):
+            x_copy(j, kind).wait_send()
 
 
 def local(hidden, targets, lengths, head):
-    aux = jnp.concatenate(
-        [
-            jnp.pad(targets, (0, 128 - HOME)).reshape(1, 128),
-            jnp.broadcast_to(lengths.reshape(1, 1), (7, 128)),
-        ]
-    )
     bf16, f32, i32 = jnp.bfloat16, jnp.float32, jnp.int32
     vmem = pl.BlockSpec(memory_space=pltpu.VMEM)
+    smem = pl.BlockSpec(memory_space=pltpu.SMEM)
     dma = pltpu.SemaphoreType.DMA
     grad, loss = pl.pallas_call(
         kernel,
         out_shape=(
             jax.ShapeDtypeStruct((HOME, WIDTH), bf16),
-            jax.ShapeDtypeStruct((8, 128), f32),
+            jax.ShapeDtypeStruct((1, 1), f32),
         ),
-        in_specs=[vmem] * 3,
-        out_specs=(vmem, vmem),
+        in_specs=[vmem, vmem, smem, vmem],
+        out_specs=(vmem, smem),
         scratch_shapes=[
             pltpu.VMEM((WIDTH, LEVELS), bf16),
             pltpu.VMEM((ROWS, WIDTH), bf16),
-            pltpu.VMEM((8, 8, 128), i32),
+            pltpu.VMEM((8, 1, HOME), i32),
             pltpu.VMEM((ROWS, LEVELS), f32),
             pltpu.VMEM((ROWS, LEVELS), bf16),
-            pltpu.VMEM((CHUNKS, ROWS, CHUNK), bf16),
-            pltpu.VMEM((CHUNKS, 128, CHUNK), bf16),
-            pltpu.VMEM((CHUNKS, 128, CHUNK), bf16),
-            pltpu.VMEM((CHUNKS, 128, CHUNK), bf16),
-            pltpu.VMEM((CHUNKS, 128, CHUNK), bf16),
-            pltpu.VMEM((CHUNKS, HOME, CHUNK), bf16),
-            pltpu.VMEM((CHUNKS, HOME, CHUNK), bf16),
-            pltpu.VMEM((CHUNKS, HOME, CHUNK), f32),
+            pltpu.VMEM((CHUNKS, 4, 2, HOME, CHUNK), bf16),
+            pltpu.VMEM((XC, 2, HOME, CHUNK), bf16),
+            pltpu.VMEM((XC, 2, HOME, CHUNK), bf16),
+            pltpu.VMEM((XC, 2, HOME, CHUNK), bf16),
+            pltpu.VMEM((XC, 2, HOME, CHUNK), bf16),
+            pltpu.VMEM((XC, HOME, CHUNK), bf16),
+            pltpu.VMEM((XC, HOME, CHUNK), bf16),
+            pltpu.VMEM((YC, 4, HOME, CHUNK), bf16),
+            pltpu.VMEM((YC, 2, HOME, CHUNK), bf16),
+            pltpu.VMEM((YC, HOME, CHUNK), bf16),
+            pltpu.VMEM((YC, HOME, CHUNK), bf16),
+            pltpu.VMEM((YC, HOME, CHUNK), bf16),
+            pltpu.VMEM((YC, HOME, CHUNK), bf16),
             pltpu.VMEM((8, 3, 8, 128), f32),
             pltpu.VMEM((8, 128), f32),
             pltpu.VMEM((2, 12, 8, 128), f32),
@@ -480,14 +533,15 @@
             dma((7,)), dma((7,)),
             dma((7,)), dma((7,)),
             dma((2, 9)), dma((2, 9)),
-            dma((4, CHUNKS)), dma((4, CHUNKS)),
+            dma((4, XC)), dma((4, XC)),
+            dma((4, YC)), dma((4, YC)),
             dma((3,)),
         ],
         compiler_params=pltpu.CompilerParams(
             collective_id=0, has_side_effects=True, vmem_limit_bytes=58 * 2**20
         ),
-    )(hidden, aux, head)
-    return grad, loss[0, 0]
+    )(hidden, targets.reshape(1, HOME), lengths, head)
+    return grad, loss.reshape(())
 
 
 def solution(mesh):

time: 132 us -> 112 us (0.85)
  Pallas kernels: 127 us -> 107 us
  local copies, waits for them, and re-layouts: 4.21 us -> 1.77 us
  between operations: 1.29 us -> 3.04 us
    pallas_call x1, Pallas kernels: 127 us -> 107 us  [local(): pl.pallas_call(kernel, out_shape=(jax.ShapeDtypeStruct((HOME, WIDTH), bf1...]
where the time goes in v2:
time: 112 us; the launch traced here: 111 us
  Pallas kernels  107 us (96%)
  between operations  3.04 us (3%)
  local copies, waits for them, and re-layouts  1.77 us (2%)
    pallas_call x1, Pallas kernels, local(): pl.pallas_call(kernel, out_shape=(jax.ShapeDtypeStruct((HOME, WIDTH), bf1...  107 us

profile of v2, /device:TPU:4, one launch (start us, length us, event | category | flops | bytes accessed | tf_op | source)
XLA Modules:
  0.0 111.4 jit_solution(7850132823067125608)
XLA Ops:
  1.3 106.6 %shard_map.59 = (bf16[64,3072]{1,0:T(8,128)(2,1)}, f32[1,1]{1,0:T(1,128)}) custom-call(bf16[64,3072]{1,0:T(8,128)(2,1)} %hid_ref.1, s32[1,64]{1,0:T(1,128)} %bitcast.2, s32[1]{0:T(128)S(6)} %copy.8.len_ref, bf16[96,2048]{1,0:T(8,128)(2,1)} %head_ref.1), custom_call_target="tpu_custom_call" | custom-call | tf_op jit(solution)/shard_map/pallas_call | solution.py:499
  107.8 1.8 %copy.9 = bf16[64,3072]{1,0:T(8,128)(2,1)} copy(bf16[64,3072]{1,0:T(8,128)(2,1)} %get-tuple-element.8) | data formatting | bytes 786432

commit v3 on v2

--- a/solution.py
+++ b/solution.py
@@ -447,41 +447,41 @@
         x_copy(j, 3).wait_recv()
         write(j, x_sum(j, yl) + f32(YR[j - YC]))
 
+    compute(5)
+    x_first(5)
+    compute(3)
+    x_first(3)
+    compute(2)
+    x_first(2)
+    compute(1)
+    y_copy(1, 0).start()
+    compute(4)
+    x_first(4)
+    x_second(3)
+    x_second(5)
+    sum_stage(1, 1)
     compute(0)
     y_copy(0, 0).start()
-    compute(1)
-    y_copy(1, 0).start()
-    compute(2)
-    x_first(2)
-    compute(3)
-    x_first(3)
-    sum_stage(1, 1)
-    compute(4)
-    compute(5)
     x_second(2)
-    y_first(0)
-    x_first(4)
-    x_second(3)
-    sum_stage(1, 2)
-    y_second(0)
-    x_first(5)
+    x_second(4)
     y_first(1)
-    x_second(4)
     x_third(2)
     x_third(3)
+    sum_stage(1, 2)
+    y_first(0)
+    x_third(4)
     y_second(1)
-    x_second(5)
-    y_last(0)
-    x_third(4)
+    x_third(5)
     x_last(2)
-    x_last(3)
-    x_third(5)
+    y_second(0)
     y_last(1)
     x_last(4)
+    x_last(5)
+    x_last(3)
 
     loss = sum_stage(1, 3) / count_tile
     loss_ref[0, 0] = loss[0, 0]
-    x_last(5)
+    y_last(0)
     for copy in sent:
         copy.wait_send()
     for kind in range(4):

time: 112 us -> 108 us (0.964)
  Pallas kernels: 107 us -> 103 us
    pallas_call x1, Pallas kernels: 107 us -> 103 us  [local(): pl.pallas_call(kernel, out_shape=(jax.ShapeDtypeStruct((HOME, WIDTH), bf1...]
where the time goes in v3:
time: 108 us
  Pallas kernels  103 us (95%)
  between operations  3.04 us (3%)
  local copies, waits for them, and re-layouts  1.77 us (2%)
    pallas_call x1, Pallas kernels, local(): pl.pallas_call(kernel, out_shape=(jax.ShapeDtypeStruct((HOME, WIDTH), bf1...  103 us

profile of v3, /device:TPU:4, one launch (start us, length us, event | category | flops | bytes accessed | tf_op | source)
XLA Modules:
  0.0 107.6 jit_solution(6301764158591653817)
XLA Ops:
  1.3 102.8 %shard_map.59 = (bf16[64,3072]{1,0:T(8,128)(2,1)}, f32[1,1]{1,0:T(1,128)}) custom-call(bf16[64,3072]{1,0:T(8,128)(2,1)} %hid_ref.1, s32[1,64]{1,0:T(1,128)} %bitcast.2, s32[1]{0:T(128)S(6)} %copy.8.len_ref, bf16[96,2048]{1,0:T(8,128)(2,1)} %head_ref.1), custom_call_target="tpu_custom_call" | custom-call | tf_op jit(solution)/shard_map/pallas_call | solution.py:499
  104.1 1.8 %copy.9 = bf16[64,3072]{1,0:T(8,128)(2,1)} copy(bf16[64,3072]{1,0:T(8,128)(2,1)} %get-tuple-element.8) | data formatting | bytes 786432

commit v4 on v3

--- a/solution.py
+++ b/solution.py
@@ -19,15 +19,19 @@
 HEAD_ROWS = 96
 PART = 48
 HALF = LEVELS // 2
+SUB = 32
 CHUNKS = 6
-CHUNK = WIDTH // CHUNKS
+CHUNK = WIDTH // 3
 QUAD = 768
 XC, YC = 4, 2
+HALF_OF = (1, 0, 1, 0, 1, 0)
+COLUMN_OF = (2, 2, 0, 1, 1, 0)
+TURN = (-1, 1, 1, -1, -1, 1)
 
 
 def kernel(
     hid_ref, tgt_ref, len_ref, head_ref, grad_ref, loss_ref,
-    H, X, A, L, G, PT, XR1, XR2, XR3, XS2, SY, YR, YF, SA, YR1, YR2, YR3, YS2, ST, LS, SB,
+    H, X, A, L, G, PT, XR1, XR2, XR3, XS2, SY, YR, YF, SA, YR1, YR2, YR3, YS2, ST, HT, LS, SB,
     zs, zr, ys, yr, cs, cr, hs, hr, as_, ar, ts, tr, ss, sr, xs, xr, ws, wr, ls,
 ):
     yh, z, c, x, yl = (lax.axis_index(name) for name in AXES)
@@ -72,7 +76,7 @@
 
     own_copies = [
         pltpu.make_async_copy(head_ref, head_at(yh, z, c, 0, HEAD_ROWS), ls.at[0]),
-        pltpu.make_async_copy(hid_ref, X.at[pl.ds(pl.multiple_of(me * HOME, HOME), HOME), :], ls.at[1]),
+        pltpu.make_async_copy(hid_ref, X.at[:, me], ls.at[1]),
         pltpu.make_async_copy(tgt_ref, A.at[me], ls.at[2]),
     ]
     for copy in own_copies:
@@ -167,9 +171,7 @@
         return head_at(oyh, zdev(-DIRS[dr] * step), cc, PART, PART, lanes_of(step, dr))
 
     def hid_at(v, half=None):
-        if half is None:
-            return X.at[pl.ds(pl.multiple_of(v * HOME, HOME), HOME), :]
-        return X.at[pl.ds(pl.multiple_of(v * HOME + half * 32, 32), 32), :]
+        return X.at[:, v] if half is None else X.at[half, v]
 
     sum_copy(0, 0).start()
     for n, (dx, dy) in enumerate(vocab_peers):
@@ -227,22 +229,26 @@
             n = 5 + 2 * kind + dr
             remote(half, half, hs.at[n], hr.at[n], x=xdev(DIRS[dr])).wait_recv()
 
-    def multiply(quad, ring, fresh=False):
+    def multiply(quad, ring, fresh=False, half=None):
         start = pl.multiple_of(ring * 1536 + quad * QUAD, 256)
+        halves = slice(0, 2) if half is None else slice(half, half + 1)
+        rows = slice(halves.start * 256, halves.stop * 256)
+        width = 512 if half is None else 1024
 
         def tile(n, carry):
-            at = pl.ds(pl.multiple_of(n * 512, 512), 512)
+            at = pl.ds(pl.multiple_of(n * width, width), width)
             part = jnp.dot(
-                X[:, pl.ds(start, QUAD)], H[pl.ds(start, QUAD), at],
+                X[halves, :, :, pl.ds(start, QUAD)].reshape(-1, QUAD),
+                H[pl.ds(start, QUAD), at],
                 preferred_element_type=jnp.float32,
             )
             if fresh:
-                L[:, at] = part
+                L[rows, at] = part
             else:
-                L[:, at] += part
+                L[rows, at] += part
             return carry
 
-        lax.fori_loop(0, LEVELS // 512, tile, 0)
+        lax.fori_loop(0, LEVELS // width, tile, 0)
 
     near = lax.div(z, 4)
     far = 1 - near
@@ -299,12 +305,12 @@
     take_y(4)
     count_tile = sum_stage(0, 3)
     take_c(4, False)
-    multiply(far, oyh)
 
     base = me * LEVELS
-    lane = lax.broadcasted_iota(jnp.int32, (HOME, 128), 1)
-    eye = lane == lax.broadcasted_iota(jnp.int32, (HOME, 128), 0)
-    level = lax.broadcasted_iota(jnp.int32, (HOME, LEVELS), 1)
+    lane = lax.broadcasted_iota(jnp.int32, (SUB, 128), 1)
+    eye = lane == lax.broadcasted_iota(jnp.int32, (SUB, 128), 0)
+    level = lax.broadcasted_iota(jnp.int32, (SUB, LEVELS), 1)
+    place64 = lax.broadcasted_iota(jnp.int32, (SUB, HOME), 1)
 
     def to_row(column):
         return jnp.sum(jnp.where(eye, column, 0.0), axis=0, keepdims=True)
@@ -312,75 +318,117 @@
     def to_column(row):
         return jnp.sum(jnp.where(eye, row, 0.0), axis=1, keepdims=True)
 
-    def target_of(v):
+    def target_of(half, v):
         row = A[v].astype(jnp.float32)
-        return jnp.sum(jnp.where(eye[:, :HOME], row, 0.0), axis=1, keepdims=True).astype(jnp.int32) - base
-
-    def rows_of(v):
-        return pl.ds(pl.multiple_of(v * HOME, HOME), HOME)
-
-    def statistics(v, carry):
-        logits = L[rows_of(v), :]
-        top = jnp.max(logits, axis=1, keepdims=True)
-        total = jnp.sum(jnp.exp(logits - top), axis=1, keepdims=True)
-        hit = jnp.sum(jnp.where(level == target_of(v), logits, 0.0), axis=1, keepdims=True)
-        for n, column in enumerate((top, total, hit)):
-            ST[me, n, pl.ds(v, 1), :] = to_row(column)
-        return carry
-
-    lax.fori_loop(0, 8, statistics, 0)
-    for n, (dx, dy) in enumerate(vocab_peers):
-        send(remote(ST.at[me], ST.at[me], ts.at[n], tr.at[n], **vpeer(dx, dy)))
-    for n, (dx, dy) in enumerate(vocab_peers):
-        there = ST.at[vindex(dx, dy)]
-        remote(ST.at[me], there, ts.at[n], tr.at[n], **vpeer(dx, dy)).wait_recv()
-
-    top = ST[0, 0]
-    for v in range(1, 8):
-        top = jnp.maximum(top, ST[v, 0])
-    total = jnp.zeros((8, 128), jnp.float32)
-    hit = jnp.zeros((8, 128), jnp.float32)
-    for v in range(8):
-        total = total + ST[v, 1] * jnp.exp(ST[v, 0] - top)
-        hit = hit + ST[v, 2]
-    log_total = top + jnp.log(total)
-    LS[...] = log_total
+        here = place64 == lax.broadcasted_iota(jnp.int32, (SUB, HOME), 0) + half * SUB
+        column = jnp.sum(jnp.where(here, row, 0.0), axis=1, keepdims=True)
+        return column.astype(jnp.int32) - base
+
+    def rows_of(half, v):
+        return pl.ds(pl.multiple_of(half * 256 + v * SUB, SUB), SUB)
+
+    def stat_copy(half, n, who):
+        ref = ST.at[half, who] if half < 2 else HT.at[who]
+        mine = ST.at[half, me] if half < 2 else HT.at[me]
+        return remote(mine, ref, ts.at[half, n], tr.at[half, n], **vpeer(*vocab_peers[n]))
+
+    def stat_send(half):
+        for n in range(7):
+            send(stat_copy(half, n, me))
+
+    def stat_wait(half):
+        for n, (dx, dy) in enumerate(vocab_peers):
+            stat_copy(half, n, vindex(dx, dy)).wait_recv()
+
+    def statistics(half):
+        def block(v, carry):
+            logits = L[rows_of(half, v), :]
+            top = jnp.max(logits, axis=1, keepdims=True)
+            total = jnp.sum(jnp.exp(logits - top), axis=1, keepdims=True)
+            ST[half, me, 0, pl.ds(v, 1), :] = to_row(top)
+            ST[half, me, 1, pl.ds(v, 1), :] = to_row(total)
+            return carry
+
+        for v in range(8):
+            block(v, 0)
+        stat_send(half)
+
+    for half in range(2):
+        multiply(far, oyh, half=half)
+        statistics(half)
+
+    def hits(half):
+        def block(v, carry):
+            found = jnp.where(level == target_of(half, v), L[rows_of(half, v), :], 0.0)
+            HT[me, half, pl.ds(v, 1), :] = to_row(jnp.sum(found, axis=1, keepdims=True))
+            return carry
+
+        for v in range(8):
+            block(v, 0)
+
+    hits(0)
+    hits(1)
+    stat_send(2)
 
     length = len_ref[0]
-    lane8 = lax.broadcasted_iota(jnp.int32, (8, 128), 1)
-    place = lax.broadcasted_iota(jnp.int32, (8, 128), 0) * HOME + lane8
-    counted = (lane8 < HOME) & (place < length)
-    row_loss = jnp.where(counted, log_total - hit, 0.0)
-    clip_loss = jnp.sum(jnp.sum(row_loss, axis=1, keepdims=True), axis=0, keepdims=True)
-    SB[1, 0] = jnp.broadcast_to(clip_loss, (8, 128))
     count = count_tile[0:1, 0:1]
 
-    def gradient(v, carry):
-        place = v * HOME + lax.broadcasted_iota(jnp.int32, (HOME, 1), 0)
-        weight = jnp.where(place < length, 1.0, 0.0) / count
-        share = jnp.exp(L[rows_of(v), :] - to_column(LS[pl.ds(v, 1), :]))
-        share = share - jnp.where(level == target_of(v), 1.0, 0.0)
-        G[rows_of(v), :] = (weight * share).astype(jnp.bfloat16)
-        return carry
-
-    lax.fori_loop(0, 8, gradient, 0)
-    sum_copy(1, 0).start()
+    def gradient(half):
+        stat_wait(half)
+        top = ST[half, 0, 0]
+        for v in range(1, 8):
+            top = jnp.maximum(top, ST[half, v, 0])
+        total = jnp.zeros((8, 128), jnp.float32)
+        for v in range(8):
+            total = total + ST[half, v, 1] * jnp.exp(ST[half, v, 0] - top)
+        LS[half] = top + jnp.log(total)
+
+        def block(v, carry):
+            place = v * HOME + half * SUB + lax.broadcasted_iota(jnp.int32, (SUB, 1), 0)
+            weight = jnp.where(place < length, 1.0, 0.0) / count
+            share = jnp.exp(L[rows_of(half, v), :] - to_column(LS[half, pl.ds(v, 1), :]))
+            share = share - jnp.where(level == target_of(half, v), 1.0, 0.0)
+            G[rows_of(half, v), :] = (weight * share).astype(jnp.bfloat16)
+            return carry
+
+        for v in range(8):
+            block(v, 0)
+
+    def loss_start():
+        stat_wait(2)
+        lane8 = lax.broadcasted_iota(jnp.int32, (8, 128), 1)
+        block8 = lax.broadcasted_iota(jnp.int32, (8, 128), 0)
+        row_loss = jnp.zeros((8, 128), jnp.float32)
+        for half in range(2):
+            hit = HT[0, half]
+            for v in range(1, 8):
+                hit = hit + HT[v, half]
+            counted = (lane8 < SUB) & (block8 * HOME + half * SUB + lane8 < length)
+            row_loss = row_loss + jnp.where(counted, LS[half] - hit, 0.0)
+        clip_loss = jnp.sum(jnp.sum(row_loss, axis=1, keepdims=True), axis=0, keepdims=True)
+        SB[1, 0] = jnp.broadcast_to(clip_loss, (8, 128))
+        sum_copy(1, 0).start()
+
+    gradient(0)
 
     def f32(value):
         return value.astype(jnp.float32)
 
     def turn(j):
-        return 1 if j % 2 else -1
+        return TURN[j]
+
+    def columns(j):
+        return pl.ds(COLUMN_OF[j] * CHUNK, CHUNK)
 
     def compute(j):
-        rows = pl.ds(j * CHUNK, CHUNK)
         product = lax.dot_general(
-            G[...], H[rows, :], (((1,), (1,)), ((), ())), preferred_element_type=jnp.float32
+            G[pl.ds(HALF_OF[j] * 256, 256), :], H[columns(j), :], (((1,), (1,)), ((), ())),
+            preferred_element_type=jnp.float32,
         )
-        PT[j] = product.astype(jnp.bfloat16).reshape(4, 2, HOME, CHUNK)
+        PT[j] = product.astype(jnp.bfloat16).reshape(4, 2, SUB, CHUNK)
 
     def write(j, value):
-        grad_ref[:, j * CHUNK : (j + 1) * CHUNK] = value.astype(jnp.bfloat16)
+        grad_ref[HALF_OF[j], :, columns(j)] = value.astype(jnp.bfloat16)
 
     def y_copy(j, kind):
         d = turn(j)
@@ -447,37 +495,39 @@
         x_copy(j, 3).wait_recv()
         write(j, x_sum(j, yl) + f32(YR[j - YC]))
 
+    compute(3)
+    x_first(3)
     compute(5)
     x_first(5)
-    compute(3)
-    x_first(3)
+    compute(1)
+    y_copy(1, 0).start()
+    gradient(1)
+    compute(4)
+    x_first(4)
+    compute(0)
+    y_copy(0, 0).start()
     compute(2)
     x_first(2)
-    compute(1)
-    y_copy(1, 0).start()
-    compute(4)
-    x_first(4)
+    loss_start()
     x_second(3)
     x_second(5)
-    sum_stage(1, 1)
-    compute(0)
-    y_copy(0, 0).start()
-    x_second(2)
     x_second(4)
     y_first(1)
-    x_third(2)
+    x_second(2)
     x_third(3)
-    sum_stage(1, 2)
+    x_third(5)
+    sum_stage(1, 1)
     y_first(0)
     x_third(4)
+    x_third(2)
+    x_last(3)
     y_second(1)
-    x_third(5)
+    y_second(0)
+    x_last(5)
+    sum_stage(1, 2)
+    x_last(4)
+    y_last(1)
     x_last(2)
-    y_second(0)
-    y_last(1)
-    x_last(4)
-    x_last(5)
-    x_last(3)
 
     loss = sum_stage(1, 3) / count_tile
     loss_ref[0, 0] = loss[0, 0]
@@ -499,39 +549,40 @@
     grad, loss = pl.pallas_call(
         kernel,
         out_shape=(
-            jax.ShapeDtypeStruct((HOME, WIDTH), bf16),
+            jax.ShapeDtypeStruct((2, SUB, WIDTH), bf16),
             jax.ShapeDtypeStruct((1, 1), f32),
         ),
         in_specs=[vmem, vmem, smem, vmem],
         out_specs=(vmem, smem),
         scratch_shapes=[
             pltpu.VMEM((WIDTH, LEVELS), bf16),
-            pltpu.VMEM((ROWS, WIDTH), bf16),
+            pltpu.VMEM((2, 8, SUB, WIDTH), bf16),
             pltpu.VMEM((8, 1, HOME), i32),
             pltpu.VMEM((ROWS, LEVELS), f32),
             pltpu.VMEM((ROWS, LEVELS), bf16),
-            pltpu.VMEM((CHUNKS, 4, 2, HOME, CHUNK), bf16),
-            pltpu.VMEM((XC, 2, HOME, CHUNK), bf16),
-            pltpu.VMEM((XC, 2, HOME, CHUNK), bf16),
-            pltpu.VMEM((XC, 2, HOME, CHUNK), bf16),
-            pltpu.VMEM((XC, 2, HOME, CHUNK), bf16),
-            pltpu.VMEM((XC, HOME, CHUNK), bf16),
-            pltpu.VMEM((XC, HOME, CHUNK), bf16),
-            pltpu.VMEM((YC, 4, HOME, CHUNK), bf16),
-            pltpu.VMEM((YC, 2, HOME, CHUNK), bf16),
-            pltpu.VMEM((YC, HOME, CHUNK), bf16),
-            pltpu.VMEM((YC, HOME, CHUNK), bf16),
-            pltpu.VMEM((YC, HOME, CHUNK), bf16),
-            pltpu.VMEM((YC, HOME, CHUNK), bf16),
-            pltpu.VMEM((8, 3, 8, 128), f32),
-            pltpu.VMEM((8, 128), f32),
+            pltpu.VMEM((CHUNKS, 4, 2, SUB, CHUNK), bf16),
+            pltpu.VMEM((XC, 2, SUB, CHUNK), bf16),
+            pltpu.VMEM((XC, 2, SUB, CHUNK), bf16),
+            pltpu.VMEM((XC, 2, SUB, CHUNK), bf16),
+            pltpu.VMEM((XC, 2, SUB, CHUNK), bf16),
+            pltpu.VMEM((XC, SUB, CHUNK), bf16),
+            pltpu.VMEM((XC, SUB, CHUNK), bf16),
+            pltpu.VMEM((YC, 4, SUB, CHUNK), bf16),
+            pltpu.VMEM((YC, 2, SUB, CHUNK), bf16),
+            pltpu.VMEM((YC, SUB, CHUNK), bf16),
+            pltpu.VMEM((YC, SUB, CHUNK), bf16),
+            pltpu.VMEM((YC, SUB, CHUNK), bf16),
+            pltpu.VMEM((YC, SUB, CHUNK), bf16),
+            pltpu.VMEM((2, 8, 2, 8, 128), f32),
+            pltpu.VMEM((8, 2, 8, 128), f32),
+            pltpu.VMEM((2, 8, 128), f32),
             pltpu.VMEM((2, 12, 8, 128), f32),
             dma((2, 4, 3)), dma((2, 4, 3)),
             dma((10,)), dma((10,)),
             dma((35,)), dma((35,)),
             dma((9,)), dma((9,)),
             dma((7,)), dma((7,)),
-            dma((7,)), dma((7,)),
+            dma((3, 7)), dma((3, 7)),
             dma((2, 9)), dma((2, 9)),
             dma((4, XC)), dma((4, XC)),
             dma((4, YC)), dma((4, YC)),
@@ -540,8 +591,8 @@
         compiler_params=pltpu.CompilerParams(
             collective_id=0, has_side_effects=True, vmem_limit_bytes=58 * 2**20
         ),
-    )(hidden, targets.reshape(1, HOME), lengths, head)
-    return grad, loss.reshape(())
+    )(hidden.reshape(2, SUB, WIDTH), targets.reshape(1, HOME), lengths, head)
+    return grad.reshape(HOME, WIDTH), loss.reshape(())
 
 
 def solution(mesh):

time: 108 us -> 106 us (0.981)
  Pallas kernels: 103 us -> 100 us
    pallas_call x1, Pallas kernels: 103 us -> 100 us  [local(): pl.pallas_call(kernel, out_shape=(jax.ShapeDtypeStruct((2, SUB, WIDTH), b...]
where the time goes in v4:
time: 106 us; the launch traced here: 105 us
  Pallas kernels  100 us (94%)
  between operations  3.04 us (3%)
  local copies, waits for them, and re-layouts  1.77 us (2%)
    pallas_call x1, Pallas kernels, local(): pl.pallas_call(kernel, out_shape=(jax.ShapeDtypeStruct((2, SUB, WIDTH), b...  100 us

profile of v4, /device:TPU:4, one launch (start us, length us, event | category | flops | bytes accessed | tf_op | source)
XLA Modules:
  0.0 105.0 jit_solution(4742520368781254314)
XLA Ops:
  1.3 100.2 %shard_map.59 = (bf16[2,32,3072]{2,1,0:T(8,128)(2,1)}, f32[1,1]{1,0:T(1,128)}) custom-call(bf16[2,32,3072]{2,1,0:T(8,128)(2,1)} %bitcast.4, s32[1,64]{1,0:T(1,128)} %bitcast.6, s32[1]{0:T(128)S(6)} %copy.8.len_ref, bf16[96,2048]{1,0:T(8,128)(2,1)} %head_ref.1), custom_call_target="tpu_custom_call" | custom-call | tf_op jit(solution)/shard_map/pallas_call | solution.py:549
  101.5 1.8 %copy.9 = bf16[64,3072]{1,0:T(8,128)(2,1)} copy(bf16[64,3072]{1,0:T(8,128)(2,1)} %bitcast.5) | data formatting | bytes 786432

commit v5 on v4

--- a/solution.py
+++ b/solution.py
@@ -26,7 +26,7 @@
 XC, YC = 4, 2
 HALF_OF = (1, 0, 1, 0, 1, 0)
 COLUMN_OF = (2, 2, 0, 1, 1, 0)
-TURN = (-1, 1, 1, -1, -1, 1)
+TURN = (-1, 1, -1, 1, -1, 1)
 
 
 def kernel(
@@ -499,39 +499,39 @@
     x_first(3)
     compute(5)
     x_first(5)
+    gradient(1)
+    compute(0)
+    y_copy(0, 0).start()
+    compute(4)
+    x_first(4)
+    compute(2)
+    x_first(2)
     compute(1)
     y_copy(1, 0).start()
-    gradient(1)
-    compute(4)
-    x_first(4)
-    compute(0)
-    y_copy(0, 0).start()
-    compute(2)
-    x_first(2)
     loss_start()
-    x_second(3)
     x_second(5)
     x_second(4)
+    x_second(3)
+    x_second(2)
+    y_first(0)
     y_first(1)
-    x_second(2)
-    x_third(3)
     x_third(5)
     sum_stage(1, 1)
-    y_first(0)
     x_third(4)
+    x_third(3)
     x_third(2)
+    y_second(0)
+    y_second(1)
+    x_last(5)
+    x_last(4)
+    sum_stage(1, 2)
+    y_last(0)
     x_last(3)
-    y_second(1)
-    y_second(0)
-    x_last(5)
-    sum_stage(1, 2)
-    x_last(4)
-    y_last(1)
     x_last(2)
 
     loss = sum_stage(1, 3) / count_tile
     loss_ref[0, 0] = loss[0, 0]
-    y_last(0)
+    y_last(1)
     for copy in sent:
         copy.wait_send()
     for kind in range(4):

time: 106 us -> 105 us (level)
  Pallas kernels: 100 us -> 98.9 us
    pallas_call x1, Pallas kernels: 100 us -> 98.9 us  [local(): pl.pallas_call(kernel, out_shape=(jax.ShapeDtypeStruct((2, SUB, WIDTH), b...]
where the time goes in v5:
time: 105 us; the launch traced here: 104 us
  Pallas kernels  98.9 us (94%)
  between operations  3.04 us (3%)
  local copies, waits for them, and re-layouts  1.77 us (2%)
    pallas_call x1, Pallas kernels, local(): pl.pallas_call(kernel, out_shape=(jax.ShapeDtypeStruct((2, SUB, WIDTH), b...  98.9 us

profile of v5, /device:TPU:4, one launch (start us, length us, event | category | flops | bytes accessed | tf_op | source)
XLA Modules:
  0.0 103.7 jit_solution(16818176317857652448)
XLA Ops:
  1.3 98.9 %shard_map.59 = (bf16[2,32,3072]{2,1,0:T(8,128)(2,1)}, f32[1,1]{1,0:T(1,128)}) custom-call(bf16[2,32,3072]{2,1,0:T(8,128)(2,1)} %bitcast.4, s32[1,64]{1,0:T(1,128)} %bitcast.6, s32[1]{0:T(128)S(6)} %copy.8.len_ref, bf16[96,2048]{1,0:T(8,128)(2,1)} %head_ref.1), custom_call_target="tpu_custom_call" | custom-call | tf_op jit(solution)/shard_map/pallas_call | solution.py:549
  100.2 1.8 %copy.9 = bf16[64,3072]{1,0:T(8,128)(2,1)} copy(bf16[64,3072]{1,0:T(8,128)(2,1)} %bitcast.5) | data formatting | bytes 786432
